TPU v7x, 32 devices: a whole 2x2x4 slice. The times are simulated.
32 devices in a mesh: row: 8 (over z, x), col: 4 (over y, core), ga: 1.
Axes of the slice: x: 2, y: 2, z: 4, core: 2. Of those that a mesh axis runs over, the one named last changes fastest.
Arguments:
- pair_density: float32 [512, 24, 3072], P('row', None, 'ga'), may hold values from -6 to 6
- coulomb: float32 [3072], P('ga'), may hold values from 0.1 to 2
Outputs:
- kernel: float32 [12288, 12288], P('row', 'col')
All inputs are finite; a program needn't handle non-finite values.
Results may differ from a plain program's by a relative error of at most 0.00011.
Values sent between devices are 32-bit elements; how exact they have to be, the bound alone decides.
A program may use at most 192 MiB of HBM per device.

v0:
```python
import functools

import jax
import jax.numpy as jnp
from jax import lax
from jax.sharding import PartitionSpec as P

LANES = 128
SHARES = (4, 4, 4, 4, 4, 2, 2)


def contract(left_rows, right_rows):
    return lax.dot_general(
        left_rows,
        right_rows,
        (((1,), (1,)), ((), ())),
        precision=lax.Precision.HIGH,
        preferred_element_type=jnp.float32,
    )


def widths_of(total):
    units, shares = total // LANES, sum(SHARES)
    cuts, seen = [0], 0
    for share in SHARES:
        seen += share
        cuts.append(units * seen // shares * LANES)
    cuts[-1] = total
    return [(a, b) for a, b in zip(cuts, cuts[1:]) if b > a]


def spread(rows, row_count, col_count):
    here_row, here_col = lax.axis_index("row"), lax.axis_index("col")
    away = jnp.bitwise_xor(here_col, here_row % col_count)
    bit = col_count // 2
    while bit:
        pairs = []
        for r in range(row_count):
            for c in range(col_count):
                if (c ^ (r % col_count)) % (2 * bit) == 0:
                    pairs.append((r * col_count + c, r * col_count + (c ^ bit)))
        got = lax.ppermute(rows, ("row", "col"), pairs)
        rows = jnp.where(away % (2 * bit) == bit, got, rows)
        bit //= 2
    return rows


def local(pair_density, coulomb):
    row_count = lax.axis_size("row")
    col_count = lax.axis_size("col")
    here_row = lax.axis_index("row")
    here_col = lax.axis_index("col")
    local_k, bands, g_width = pair_density.shape
    total_k = local_k * row_count
    scale = (2.0 * coulomb) / jnp.float32(total_k)
    grouped = pair_density.reshape(local_k // col_count, col_count, bands, g_width)
    ratio = row_count // col_count
    total = None
    for start, stop in widths_of(g_width):
        width = stop - start
        own = lax.dynamic_slice(
            grouped, (0, here_col, 0, start), (local_k // col_count, 1, bands, width)
        )[:, 0]
        piece = lax.all_gather(own, "row", axis=0, tiled=True)
        paired = piece.reshape(piece.shape[0] // ratio, ratio, bands, width)
        rows = lax.dynamic_index_in_dim(paired, here_row // col_count, 1, keepdims=False)
        rows = spread(rows, row_count, col_count)
        weighted = rows.reshape(local_k * bands, width) * scale[None, start:stop]
        part = contract(weighted, piece.reshape(piece.shape[0] * bands, width))
        total = part if total is None else total + part
    return lax.psum(total, "ga")


def solution(mesh):
    placed = (P("row", None, "ga"), P("ga"))
    return jax.shard_map(
        local, mesh=mesh, in_specs=placed, out_specs=P("row", "col"), check_vma=False
    )
```

profile of v0, /device:TPU:7, one launch (start us, length us, event | category | flops | bytes accessed | tf_op | source)
XLA Modules:
  0.0 844.3 jit_solution(10733142916336064370)
XLA Ops:
  8.7 4.1 constant_dynamic-slice_fusion.5
  16.1 52.0 %all-gather.25.cloned.1.call-done = f32[128,1,24,256]{3,2,1,0:T(8,128)} async-done(((f32[16,1,24,256]{3,2,1,0:T(8,128)}), f32[128,1,24,256]{3,2,1,0:T(8,128)}) %all-gather.25.cloned.1.call-update) | async-done | bytes 3145744 | tf_op jit(solution)/shard_map/all_gather | solution.py:64
  72.1 96.0 %all-gather.15.cloned.1.call-done = f32[128,1,24,512]{3,2,1,0:T(8,128)} async-done(((f32[16,1,24,512]{3,2,1,0:T(8,128)}), f32[128,1,24,512]{3,2,1,0:T(8,128)}) %all-gather.15.cloned.1.call-update) | async-done | bytes 6291472 | tf_op jit(solution)/shard_map/all_gather | solution.py:64
  168.1 3.9 dynamic-slice_bitcast_fusion.4
  173.3 93.9 %all-gather.17.cloned.1.call-done = f32[128,1,24,512]{3,2,1,0:T(8,128)} async-done(((f32[16,1,24,512]{3,2,1,0:T(8,128)}), f32[128,1,24,512]{3,2,1,0:T(8,128)}) %all-gather.17.cloned.1.call-update) | async-done | bytes 6291472 | tf_op jit(solution)/shard_map/all_gather | solution.py:64
  267.1 3.9 dynamic-slice_bitcast_fusion.3
  272.3 54.7 %all-gather.27.cloned.1.call-done = f32[128,1,24,256]{3,2,1,0:T(8,128)} async-done(((f32[16,1,24,256]{3,2,1,0:T(8,128)}), f32[128,1,24,256]{3,2,1,0:T(8,128)}) %all-gather.27.cloned.1.call-update) | async-done | bytes 3145744 | tf_op jit(solution)/shard_map/all_gather | solution.py:64
  331.0 95.9 %all-gather.19.cloned.1.call-done = f32[128,1,24,512]{3,2,1,0:T(8,128)} async-done(((f32[16,1,24,512]{3,2,1,0:T(8,128)}), f32[128,1,24,512]{3,2,1,0:T(8,128)}) %all-gather.19.cloned.1.call-update) | async-done | bytes 6291472 | tf_op jit(solution)/shard_map/all_gather | solution.py:64
  426.8 4.0 dynamic-slice_bitcast_fusion.2
  435.3 3.5 collective-permute-start.11
  438.9 3.0 broadcast_select_fusion.5
  444.3 81.5 %all-gather.21.cloned.1.call-done = f32[128,1,24,512]{3,2,1,0:T(8,128)} async-done(((f32[16,1,24,512]{3,2,1,0:T(8,128)}), f32[128,1,24,512]{3,2,1,0:T(8,128)}) %all-gather.21.cloned.1.call-update) | async-done | bytes 6291472 | tf_op jit(solution)/shard_map/all_gather | solution.py:64
  525.8 3.9 dynamic-slice_bitcast_fusion.1
  531.0 93.8 %all-gather.23.cloned.1.call-done = f32[128,1,24,512]{3,2,1,0:T(8,128)} async-done(((f32[16,1,24,512]{3,2,1,0:T(8,128)}), f32[128,1,24,512]{3,2,1,0:T(8,128)}) %all-gather.23.cloned.1.call-update) | async-done | bytes 6291472 | tf_op jit(solution)/shard_map/all_gather | solution.py:64
  624.9 4.0 dynamic-slice_bitcast_fusion
  630.3 3.6 broadcast_select_fusion.4
  633.9 5.7 collective-permute-start.1
  639.6 4.4 broadcast_select_fusion.3
  644.0 3.0 collective-permute-start.3
  647.0 3.7 broadcast_select_fusion.2
  656.9 10.8 %fusion.7 = f32[1536,3072]{1,0:T(8,128)} fusion(f32[1536,256]{1,0:T(8,128)S(1)} %bitcast.103, f32[3072,256]{1,0:T(8,128)S(1)} %bitcast.98), kind=kOutput, calls=%fused_computation.37 | convolution fusion | flops 7247757312 | bytes 23592960 | tf_op jit(solution)/shard_map/dot_general | solution.py:13
  667.6 4.3 broadcast_select_fusion.1
  671.9 3.1 collective-permute-start.7
  675.0 4.3 broadcast_select_fusion
  679.4 3.0 collective-permute-start.9
  684.8 4.6 select_multiply_fusion.3
  693.1 18.2 %fusion.2 = f32[1536,3072]{1,0:T(8,128)} fusion(f32[1536,512]{1,0:T(8,128)S(1)} %bitcast.91, f32[3072,512]{1,0:T(8,128)S(1)} %bitcast.68), kind=kOutput, calls=%fused_computation.32 | convolution fusion | flops 14495514624 | bytes 28311552 | tf_op jit(solution)/shard_map/dot_general | solution.py:13
  711.3 20.8 %fusion.3 = f32[1536,3072]{1,0:T(8,128)} fusion(f32[1536,512]{1,0:T(8,128)} %bitcast.93, f32[3072,512]{1,0:T(8,128)S(1)} %bitcast.75), kind=kOutput, calls=%fused_computation.33 | convolution fusion | flops 14495514624 | bytes 28311552 | tf_op jit(solution)/shard_map/dot_general | solution.py:13
  735.0 18.6 %fusion.4 = f32[1536,3072]{1,0:T(8,128)} fusion(f32[1536,512]{1,0:T(8,128)S(1)} %bitcast.92, f32[3072,512]{1,0:T(8,128)S(1)} %bitcast.80), kind=kOutput, calls=%fused_computation.34 | convolution fusion | flops 14495514624 | bytes 28311552 | tf_op jit(solution)/shard_map/dot_general | solution.py:13
  753.5 18.4 %fusion.5 = f32[1536,3072]{1,0:T(8,128)} fusion(f32[1536,512]{1,0:T(8,128)S(1)} %bitcast.94, f32[3072,512]{1,0:T(8,128)S(1)} %bitcast.90), kind=kOutput, calls=%fused_computation.35 | convolution fusion | flops 14495514624 | bytes 28311552 | tf_op jit(solution)/shard_map/dot_general | solution.py:13
  774.6 18.6 %fusion.6 = f32[1536,3072]{1,0:T(8,128)} fusion(f32[1536,512]{1,0:T(8,128)S(1)} %bitcast.95, f32[3072,512]{1,0:T(8,128)S(1)} %bitcast.85), kind=kOutput, calls=%fused_computation.36 | convolution fusion | flops 14495514624 | bytes 28311552 | tf_op jit(solution)/shard_map/dot_general | solution.py:13
  793.2 43.8 %add_add_fusion = f32[1536,3072]{1,0:T(8,128)} fusion(f32[1536,3072]{1,0:T(8,128)} %fusion.7, f32[1536,3072]{1,0:T(8,128)} %fusion.6, f32[1536,3072]{1,0:T(8,128)} %fusion.5, f32[1536,3072]{1,0:T(8,128)} %fusion.4, f32[1536,3072]{1,0:T(8,128)} %fusion.2, f32[1536,3072]{1,0:T(8,128)} %fusion.3, f32[1536,256]{1,0:T(8,128)} %bitcast.102, ...), kind=kOutput, calls=%fused_computation | convolution fusion | flops 7276068864 | bytes 136839168 | tf_op jit(solution)/shard_map/dot_general | solution.py:13
  (98 shorter events, 43.0 us)
Async XLA Ops:
  6.5 61.5 %all-gather.25.cloned.1.call-start = ((), (), s32[]{:S(2)}) async-start(), calls=%async_computation.5 | async-start | bytes 3538944 | tf_op jit(solution)/shard_map/all_gather | solution.py:64
  8.6 159.4 %all-gather.15.cloned.1.call-start = ((), (), s32[]{:S(2)}) async-start(), calls=%async_computation | async-start | bytes 7077888 | tf_op jit(solution)/shard_map/all_gather | solution.py:64
  12.8 254.3 %all-gather.17.cloned.1.call-start = ((), (), s32[]{:S(2)}) async-start(), calls=%async_computation.1 | async-start | bytes 7077888 | tf_op jit(solution)/shard_map/all_gather | solution.py:64
  13.5 313.5 %all-gather.27.cloned.1.call-start = ((), (), s32[]{:S(2)}) async-start(), calls=%async_computation.6 | async-start | bytes 3538944 | tf_op jit(solution)/shard_map/all_gather | solution.py:64
  14.1 412.7 %all-gather.19.cloned.1.call-start = ((), (), s32[]{:S(2)}) async-start(), calls=%async_computation.2 | async-start | bytes 7077888 | tf_op jit(solution)/shard_map/all_gather | solution.py:64
  14.7 511.1 %all-gather.21.cloned.1.call-start = ((), (), s32[]{:S(2)}) async-start(), calls=%async_computation.3 | async-start | bytes 7077888 | tf_op jit(solution)/shard_map/all_gather | solution.py:64
  15.3 609.6 %all-gather.23.cloned.1.call-start = ((), (), s32[]{:S(2)}) async-start(), calls=%async_computation.4 | async-start | bytes 7077888 | tf_op jit(solution)/shard_map/all_gather | solution.py:64
  70.8 361.6 %collective-permute-start.10 = (f32[64,24,256]{2,1,0:T(8,128)}, f32[64,24,256]{2,1,0:T(8,128)}, u32[]{:S(2)}, u32[]{:S(2)}) collective-permute-start(f32[64,24,256]{2,1,0:T(8,128)} %dynamic-slice_bitcast_fusion.6), channel_id=1, source_target_pairs={{0,2},{5,7},{10,8},{15,13},{16,18},{21,23},{26,24},{31,29}} | collective-permute-start | bytes 4718600 | tf_op jit(solution)/shard_map/ppermute | solution.py:42
  172.0 456.9 %collective-permute-start = (f32[64,24,512]{2,1,0:T(8,128)}, f32[64,24,512]{2,1,0:T(8,128)}, u32[]{:S(2)}, u32[]{:S(2)}) collective-permute-start(f32[64,24,512]{2,1,0:T(8,128)} %dynamic-slice_bitcast_fusion.4), channel_id=1, source_target_pairs={{0,2},{5,7},{10,8},{15,13},{16,18},{21,23},{26,24},{31,29}} | collective-permute-start | bytes 9437192 | tf_op jit(solution)/shard_map/ppermute | solution.py:42
  271.0 362.9 %collective-permute-start.2 = (f32[64,24,512]{2,1,0:T(8,128)}, f32[64,24,512]{2,1,0:T(8,128)}, u32[]{:S(2)}, u32[]{:S(2)}) collective-permute-start(f32[64,24,512]{2,1,0:T(8,128)} %dynamic-slice_bitcast_fusion.3), channel_id=1, source_target_pairs={{0,2},{5,7},{10,8},{15,13},{16,18},{21,23},{26,24},{31,29}} | collective-permute-start | bytes 9437192 | tf_op jit(solution)/shard_map/ppermute | solution.py:42
  329.7 109.2 %collective-permute-start.12 = (f32[64,24,256]{2,1,0:T(8,128)}, f32[64,24,256]{2,1,0:T(8,128)}, u32[]{:S(2)}, u32[]{:S(2)}) collective-permute-start(f32[64,24,256]{2,1,0:T(8,128)} %dynamic-slice_bitcast_fusion.5), channel_id=1, source_target_pairs={{0,2},{5,7},{10,8},{15,13},{16,18},{21,23},{26,24},{31,29}} | collective-permute-start | bytes 4718600 | tf_op jit(solution)/shard_map/ppermute | solution.py:42
  430.9 213.1 %collective-permute-start.4 = (f32[64,24,512]{2,1,0:T(8,128)}, f32[64,24,512]{2,1,0:T(8,128)}, u32[]{:S(2)}, u32[]{:S(2)}) collective-permute-start(f32[64,24,512]{2,1,0:T(8,128)} %dynamic-slice_bitcast_fusion.2), channel_id=1, source_target_pairs={{0,2},{5,7},{10,8},{15,13},{16,18},{21,23},{26,24},{31,29}} | collective-permute-start | bytes 9437192 | tf_op jit(solution)/shard_map/ppermute | solution.py:42
  435.3 94.4 %collective-permute-start.11 = (f32[64,24,256]{2,1,0:T(8,128)}, f32[64,24,256]{2,1,0:T(8,128)S(1)}, u32[]{:S(2)}, u32[]{:S(2)}) collective-permute-start(f32[64,24,256]{2,1,0:T(8,128)} %broadcast_select_fusion.6), channel_id=1, source_target_pairs={{0,1},{2,3},{5,4},{7,6},{8,9},{10,11},{13,12},{15,14},{16,17},{18,... | collective-permute-start | bytes 4718600 | tf_op jit(solution)/shard_map/ppermute | solution.py:42
  441.9 208.9 %collective-permute-start.13 = (f32[64,24,256]{2,1,0:T(8,128)}, f32[64,24,256]{2,1,0:T(8,128)}, u32[]{:S(2)}, u32[]{:S(2)}) collective-permute-start(f32[64,24,256]{2,1,0:T(8,128)} %broadcast_select_fusion.5), channel_id=1, source_target_pairs={{0,1},{2,3},{5,4},{7,6},{8,9},{10,11},{13,12},{15,14},{16,17},{18,... | collective-permute-start | bytes 4718600 | tf_op jit(solution)/shard_map/ppermute | solution.py:42
  529.7 99.2 %copy-start.6 = (f32[64,24,256]{2,1,0:T(8,128)}, f32[64,24,256]{2,1,0:T(8,128)S(1)}, u32[]{:S(2)}) copy-start(f32[64,24,256]{2,1,0:T(8,128)S(1)} %collective-permute-done.11) | copy-start | bytes 4718596
  529.7 137.9 %collective-permute-start.6 = (f32[64,24,512]{2,1,0:T(8,128)}, f32[64,24,512]{2,1,0:T(8,128)}, u32[]{:S(2)}, u32[]{:S(2)}) collective-permute-start(f32[64,24,512]{2,1,0:T(8,128)} %dynamic-slice_bitcast_fusion.1), channel_id=1, source_target_pairs={{0,2},{5,7},{10,8},{15,13},{16,18},{21,23},{26,24},{31,29}} | collective-permute-start | bytes 9437192 | tf_op jit(solution)/shard_map/ppermute | solution.py:42
  624.9 14.7 %slice-start.2 = ((s8[6291456]{0:T(1024)(128)(4,1)}), s8[4194304]{0:T(1024)(128)(4,1)S(1)}, s32[]{:S(2)}) async-start(s8[6291456]{0:T(1024)(128)(4,1)} %bitcast.70), calls=%async_computation.9 | async-start | bytes 8388608
  628.9 46.1 %collective-permute-start.8 = (f32[64,24,512]{2,1,0:T(8,128)}, f32[64,24,512]{2,1,0:T(8,128)}, u32[]{:S(2)}, u32[]{:S(2)}) collective-permute-start(f32[64,24,512]{2,1,0:T(8,128)} %dynamic-slice_bitcast_fusion), channel_id=1, source_target_pairs={{0,2},{5,7},{10,8},{15,13},{16,18},{21,23},{26,24},{31,29}} | collective-permute-start | bytes 9437192 | tf_op jit(solution)/shard_map/ppermute | solution.py:42
  633.9 48.4 %collective-permute-start.1 = (f32[64,24,512]{2,1,0:T(8,128)S(1)}, f32[64,24,512]{2,1,0:T(8,128)}, u32[]{:S(2)}, u32[]{:S(2)}) collective-permute-start(f32[64,24,512]{2,1,0:T(8,128)S(1)} %broadcast_select_fusion.4), channel_id=1, source_target_pairs={{0,1},{2,3},{5,4},{7,6},{8,9},{10,11},{13,12},{15,14},{16,17},{18,... | collective-permute-start | bytes 9437192 | tf_op jit(solution)/shard_map/ppermute | solution.py:42
  644.0 40.8 %collective-permute-start.3 = (f32[64,24,512]{2,1,0:T(8,128)}, f32[64,24,512]{2,1,0:T(8,128)}, u32[]{:S(2)}, u32[]{:S(2)}) collective-permute-start(f32[64,24,512]{2,1,0:T(8,128)} %broadcast_select_fusion.3), channel_id=1, source_target_pairs={{0,1},{2,3},{5,4},{7,6},{8,9},{10,11},{13,12},{15,14},{16,17},{18,... | collective-permute-start | bytes 9437192 | tf_op jit(solution)/shard_map/ppermute | solution.py:42
  650.8 38.6 %collective-permute-start.5 = (f32[64,24,512]{2,1,0:T(8,128)S(1)}, f32[64,24,512]{2,1,0:T(8,128)S(1)}, u32[]{:S(2)}, u32[]{:S(2)}) collective-permute-start(f32[64,24,512]{2,1,0:T(8,128)S(1)} %broadcast_select_fusion.2), channel_id=1, source_target_pairs={{0,1},{2,3},{5,4},{7,6},{8,9},{10,11},{13,12},{15,14},{16,17},{18,... | collective-permute-start | bytes 9437192 | tf_op jit(solution)/shard_map/ppermute | solution.py:42
  653.9 13.7 %slice-start.10 = ((s8[6291456]{0:T(1024)(128)(4,1)}), s8[4194304]{0:T(1024)(128)(4,1)S(1)}, s32[]{:S(2)}) async-start(s8[6291456]{0:T(1024)(128)(4,1)} %bitcast.87), calls=%async_computation.17 | async-start | bytes 8388608
  653.9 21.1 %slice-start.8 = ((s8[6291456]{0:T(1024)(128)(4,1)}), s8[4194304]{0:T(1024)(128)(4,1)S(1)}, s32[]{:S(2)}) async-start(s8[6291456]{0:T(1024)(128)(4,1)} %bitcast.82), calls=%async_computation.15 | async-start | bytes 8388608
  656.8 10.8 %slice-start.11 = ((s8[6291456]{0:T(1024)(128)(4,1)}), s8[2097152]{0:T(1024)(128)(4,1)S(1)}, s32[]{:S(2)}) async-start(s8[6291456]{0:T(1024)(128)(4,1)} %bitcast.87), calls=%async_computation.18 | async-start | bytes 4194304
  656.8 18.2 %slice-start.9 = ((s8[6291456]{0:T(1024)(128)(4,1)}), s8[2097152]{0:T(1024)(128)(4,1)S(1)}, s32[]{:S(2)}) async-start(s8[6291456]{0:T(1024)(128)(4,1)} %bitcast.82), calls=%async_computation.16 | async-start | bytes 4194304
  671.9 60.2 %collective-permute-start.7 = (f32[64,24,512]{2,1,0:T(8,128)}, f32[64,24,512]{2,1,0:T(8,128)}, u32[]{:S(2)}, u32[]{:S(2)}) collective-permute-start(f32[64,24,512]{2,1,0:T(8,128)} %broadcast_select_fusion.1), channel_id=1, source_target_pairs={{0,1},{2,3},{5,4},{7,6},{8,9},{10,11},{13,12},{15,14},{16,17},{18,... | collective-permute-start | bytes 9437192 | tf_op jit(solution)/shard_map/ppermute | solution.py:42
  679.4 92.6 %collective-permute-start.9 = (f32[64,24,512]{2,1,0:T(8,128)}, f32[64,24,512]{2,1,0:T(8,128)}, u32[]{:S(2)}, u32[]{:S(2)}) collective-permute-start(f32[64,24,512]{2,1,0:T(8,128)} %broadcast_select_fusion), channel_id=1, source_target_pairs={{0,1},{2,3},{5,4},{7,6},{8,9},{10,11},{13,12},{15,14},{16,17},{18,... | collective-permute-start | bytes 9437192 | tf_op jit(solution)/shard_map/ppermute | solution.py:42
  689.4 21.9 %slice-start.4 = ((s8[6291456]{0:T(1024)(128)(4,1)}), s8[4194304]{0:T(1024)(128)(4,1)S(1)}, s32[]{:S(2)}) async-start(s8[6291456]{0:T(1024)(128)(4,1)} %bitcast.73), calls=%async_computation.11 | async-start | bytes 8388608
  693.1 18.2 %slice-start.5 = ((s8[6291456]{0:T(1024)(128)(4,1)}), s8[2097152]{0:T(1024)(128)(4,1)S(1)}, s32[]{:S(2)}) async-start(s8[6291456]{0:T(1024)(128)(4,1)} %bitcast.73), calls=%async_computation.12 | async-start | bytes 4194304
  693.1 41.9 %slice-start.6 = ((s8[6291456]{0:T(1024)(128)(4,1)}), s8[4194304]{0:T(1024)(128)(4,1)S(1)}, s32[]{:S(2)}) async-start(s8[6291456]{0:T(1024)(128)(4,1)} %bitcast.78), calls=%async_computation.13 | async-start | bytes 8388608
  711.3 23.7 %slice-start.7 = ((s8[6291456]{0:T(1024)(128)(4,1)}), s8[2097152]{0:T(1024)(128)(4,1)S(1)}, s32[]{:S(2)}) async-start(s8[6291456]{0:T(1024)(128)(4,1)} %bitcast.78), calls=%async_computation.14 | async-start | bytes 4194304
  774.6 18.6 %copy-start.5 = (f32[128,1,24,256]{3,2,1,0:T(8,128)S(1)}, f32[128,1,24,256]{3,2,1,0:T(8,128)}, u32[]{:S(2)}) copy-start(f32[128,1,24,256]{3,2,1,0:T(8,128)} %all-gather.27.cloned.1.call-done) | copy-start | bytes 9437188
  (10 other events, 55.1 us)
Sparse Core Ops, SparseCore 0:
  9.5 58.4 all-gather.24
  70.2 97.7 all-gather.14
  170.2 96.8 all-gather.16
  269.2 57.7 all-gather.26
  329.0 97.7 all-gather.18
  428.9 96.8 all-gather.20
  528.0 96.8 all-gather.22
where the time goes:
time: 853 us; the launch traced here: 844 us
  waiting for transfers between devices  571 us (67%)
  matrix products  149 us (17%)
  other arithmetic  45.8 us (5%)
  local copies, waits for them, and re-layouts  32.5 us (4%)
  starting transfers between devices  31.7 us (4%)
  between operations  14.3 us (2%)
    all_gather x7, waiting for transfers between devices, local(): piece = lax.all_gather(own, 'row', axis=0, tiled=True)  568 us
    dot_general x7, matrix products, contract(): lax.dot_general(left_rows, right_rows, (((1,), (1,)), ((), ())), precisio...  149 us
    ppermute x14, starting transfers between devices, spread(): got = lax.ppermute(rows, ('row', 'col'), pairs)  31.5 us
    select_n x7, other arithmetic, spread(): rows = jnp.where(away % (2 * bit) == bit, got, rows)  26.2 us
    squeeze x7, local copies, waits for them, and re-layouts, local(): lax.dynamic_index_in_dim(paired, here_row // col_count, 1, keepdims=False)  25.1 us
    mul x7, other arithmetic, local(): weighted = rows.reshape(local_k * bands, width) * scale[None, start:stop]  19.5 us
  transfers between devices with their start and end apart: 21, of which 7 were waited for; matrix products, arithmetic and copies ran while one was open for 19% of the time, Pallas kernels for 0%

commit v1 on v0

v1 whole, which is shorter than its diff:
```python
import functools
import math

import jax
import jax.numpy as jnp
from jax import lax
from jax.experimental import pallas as pl
from jax.experimental.pallas import tpu as pltpu
from jax.sharding import PartitionSpec as P

MESH = pl.DeviceIdType.MESH
WIDTH = 256
FLIGHT = 4
SLOTS = FLIGHT + 2
TILE = 512


def ring_at(place, count):
    far = place // (count // 2)
    return (1 - far) * 2 * place + far * (2 * (count - 1 - place) + 1)


def place_of(row, count):
    odd = row % 2
    return (1 - odd) * (row // 2) + odd * (count - 1 - row // 2)


def flip(col, bit):
    return col + bit * (1 - 2 * ((col // bit) % 2))


def split(x):
    high = x.astype(jnp.bfloat16)
    return high, (x - high.astype(jnp.float32)).astype(jnp.bfloat16)


def kernel(
    sizes, pair_ref, scale_ref, out_ref, right, left, total, weighted, columns,
    own_sem, ring_send, ring_recv, left_send, left_recv, out_sem, ring_free, left_free,
):
    row_count, col_count, chunks, parts = sizes
    ratio = row_count // col_count
    per_class, bands = right.shape[2], right.shape[4]
    width = right.shape[5]
    here_row, here_col = lax.axis_index("row"), lax.axis_index("col")
    place = place_of(here_row, row_count)
    ahead = ring_at((place + 1) % row_count, row_count)
    behind = ring_at((place + row_count - 1) % row_count, row_count)
    home_col, home_class = here_row % col_count, here_row // col_count
    bits = [1 << b for b in range(int(math.log2(col_count)))]
    away = 0
    for bit in bits:
        away = away + bit * (((here_col // bit) + (home_col // bit)) % 2)
    period = row_count // FLIGHT
    group = row_count // parts

    def target(e):
        return ahead if e % 2 == 0 else behind

    def source_at(e, t):
        step = row_count - t if e % 2 == 0 else t
        return ring_at((place + step) % row_count, row_count)

    def own_copies(g):
        s = g % SLOTS
        cut = pl.ds(pl.multiple_of(g * width, width), width)
        return (
            pltpu.make_async_copy(
                pair_ref.at[:, :, here_col, :, cut], right.at[s, here_row], own_sem.at[s, 0]
            ),
            pltpu.make_async_copy(
                pair_ref.at[:, home_class, home_col, :, cut], left.at[s, here_row], own_sem.at[s, 1]
            ),
        )

    def ring_copy(s, t, e, q):
        return pltpu.make_async_remote_copy(
            src_ref=right.at[s, q, :, e],
            dst_ref=right.at[s, q, :, e],
            send_sem=ring_send.at[s, e],
            recv_sem=ring_recv.at[s, t, e],
            device_id={"row": target(e)},
            device_id_type=MESH,
        )

    def left_copy(src, s, t, q, b):
        return pltpu.make_async_remote_copy(
            src_ref=src,
            dst_ref=left.at[s, q],
            send_sem=left_send.at[s, b],
            recv_sem=left_recv.at[s, t],
            device_id={"col": flip(here_col, bits[b])},
            device_id_type=MESH,
        )

    def home_source(t):
        up = home_class % 2
        return (1 - up) * source_at(0, t) + up * source_at(1, t)

    def ring_event(g, t):
        s = g % SLOTS
        if t == 0:
            for copy in own_copies(g):
                copy.wait()

            @pl.when(g >= SLOTS)
            def _():
                for e in range(min(ratio, 2)):
                    pl.semaphore_wait(ring_free.at[e], 1)

            for e in range(ratio):
                ring_copy(s, 1, e, here_row).start()
            return
        for e in range(ratio):
            q = source_at(e, t)
            ring_copy(s, t, e, q).wait_recv()
            if t < row_count - 1:
                ring_copy(s, t + 1, e, q).start()
        q = home_source(t)

        @pl.when(away == 0)
        def _():
            for b in range(len(bits)):
                if t == 1:

                    @pl.when(g >= SLOTS)
                    def _():
                        pl.semaphore_wait(left_free.at[b], 1)

                left_copy(right.at[s, q, :, home_class], s, t, q, b).start()

        if t == 1:

            @pl.when(g + 1 < chunks)
            def _():
                for copy in own_copies(g + 1):
                    copy.start()

    def relay_event(g, t):
        s = g % SLOTS
        q = home_source(t)

        @pl.when((away > 0) & (away % 2 == 0))
        def _():
            left_copy(left.at[s, q], s, t, q, 0).wait_recv()
            for b, bit in enumerate(bits):

                @pl.when(away % (2 * bit) == 0)
                def _():
                    if t == 1:

                        @pl.when(g >= SLOTS)
                        def _():
                            pl.semaphore_wait(left_free.at[b], 1)

                    left_copy(left.at[s, q], s, t, q, b).start()

    def weigh(g):
        s = g % SLOTS
        rows = per_class * bands
        scale = scale_ref[g]

        @pl.when(away % 2 == 1)
        def _():
            for t in range(1, row_count):
                left_copy(left.at[s, 0], s, t, 0, 0).wait_recv()

        def fill(read):
            def one(q, _):
                high, low = split(read(q).reshape(rows, width) * scale)
                at = pl.ds(pl.multiple_of(q * rows, rows), rows)
                weighted[at, pl.ds(0, width)] = high
                weighted[at, pl.ds(width, width)] = high
                weighted[at, pl.ds(2 * width, width)] = low
                return 0

            lax.fori_loop(0, row_count, one, 0)

        @pl.when(away == 0)
        def _():
            fill(lambda q: right[s, q, :, home_class])

        @pl.when(away > 0)
        def _():
            fill(lambda q: left[s, q])

    def product(g, p):
        s = g % SLOTS
        block = group * per_class * ratio * bands
        high, low = split(right[s, pl.ds(p * group, group)].reshape(block, width))
        columns[:, pl.ds(0, width)] = high
        columns[:, pl.ds(width, width)] = low
        columns[:, pl.ds(2 * width, width)] = high
        tile = min(TILE, weighted.shape[0])

        def one(i, _):
            at = pl.ds(pl.multiple_of(i * tile, tile), tile)
            total[p, at, :] += lax.dot_general(
                weighted[at, :],
                columns[...],
                (((1,), (1,)), ((), ())),
                preferred_element_type=jnp.float32,
            )
            return 0

        lax.fori_loop(0, weighted.shape[0] // tile, one, 0)

        @pl.when(g == chunks - 1)
        def _():
            out_copy(p).start()

    def out_copy(p):
        block = total.shape[2]
        return pltpu.make_async_copy(
            total.at[p], out_ref.at[:, pl.ds(p * block, block)], out_sem.at[p]
        )

    def retire(g):
        s = g % SLOTS
        several = right.at[s, pl.ds(0, row_count - 1), :, 0]
        for e in range(ratio):
            pltpu.make_async_copy(several, several, ring_send.at[s, e]).wait()
        for b, bit in enumerate(bits):

            @pl.when(away % (2 * bit) == 0)
            def _():
                pltpu.make_async_copy(several, several, left_send.at[s, b]).wait()

        @pl.when(g + SLOTS < chunks)
        def _():
            for e in range(min(ratio, 2)):
                pl.semaphore_signal(
                    ring_free.at[e], inc=1, device_id={"row": behind if e == 0 else ahead}, device_id_type=MESH
                )
            for b, bit in enumerate(bits):

                @pl.when(away % (2 * bit) == bit)
                def _():
                    pl.semaphore_signal(
                        left_free.at[b], inc=1, device_id={"col": flip(here_col, bit)}, device_id_type=MESH
                    )

    for copy in own_copies(0):
        copy.start()
    barrier = pltpu.get_barrier_semaphore()
    for row in (ahead, behind):
        pl.semaphore_signal(barrier, inc=1, device_id={"row": row}, device_id_type=MESH)
    for bit in bits:
        pl.semaphore_signal(barrier, inc=1, device_id={"col": flip(here_col, bit)}, device_id_type=MESH)
    pl.semaphore_wait(barrier, 2 + len(bits))

    def clear(i, _):
        for p in range(parts):
            total[p, pl.ds(pl.multiple_of(i * 8, 8), 8), :] = jnp.zeros((8, total.shape[2]), jnp.float32)
        return 0

    lax.fori_loop(0, total.shape[1] // 8, clear, 0)

    def live(g, run):
        pl.when((g >= 0) & (g < chunks))(run)

    def round_of(base, _):
        for i in range(period):
            for d in range(FLIGHT + 1):
                t = i + d * period - 1
                if 1 <= t < row_count:
                    live(base - d, functools.partial(relay_event, base - d, t))
            for d in reversed(range(FLIGHT)):
                live(base - d, functools.partial(ring_event, base - d, i + d * period))
                if d % 2 == 0:
                    g = base - FLIGHT
                    p = 2 * i + (1 - d // 2)
                    if p == 0:
                        live(g, functools.partial(weigh, g))
                    if p < parts:
                        live(g, functools.partial(product, g, p))
        live(base - FLIGHT, functools.partial(retire, base - FLIGHT))
        return 0

    lax.fori_loop(0, chunks + FLIGHT, round_of, 0)
    for p in range(parts):
        out_copy(p).wait()


def local(pair_density, coulomb):
    row_count, col_count = lax.axis_size("row"), lax.axis_size("col")
    ratio = row_count // col_count
    local_k, bands, g_width = pair_density.shape
    total_k = local_k * row_count
    per_class = local_k // row_count
    width = math.gcd(WIDTH, g_width)
    chunks = g_width // width
    m, n = local_k * bands, total_k // col_count * bands
    piece = per_class * ratio * bands
    group = 1
    while group * piece % 256:
        group *= 2
    parts = row_count // group
    scale = ((2.0 * coulomb) / jnp.float32(total_k)).reshape(chunks, 1, width)
    pair = pair_density.reshape(per_class, ratio, col_count, bands, g_width)
    nbits = int(math.log2(col_count))
    f32 = jnp.float32
    total = pl.pallas_call(
        functools.partial(kernel, (row_count, col_count, chunks, parts)),
        out_shape=jax.ShapeDtypeStruct((m, n), f32),
        in_specs=[pl.BlockSpec(memory_space=pl.ANY), pl.BlockSpec(memory_space=pltpu.VMEM)],
        out_specs=pl.BlockSpec(memory_space=pl.ANY),
        scratch_shapes=[
            pltpu.VMEM((SLOTS, row_count, per_class, ratio, bands, width), f32),
            pltpu.VMEM((SLOTS, row_count, per_class, bands, width), f32),
            pltpu.VMEM((parts, m, group * piece), f32),
            pltpu.VMEM((m, 3 * width), jnp.bfloat16),
            pltpu.VMEM((group * piece, 3 * width), jnp.bfloat16),
            pltpu.SemaphoreType.DMA((SLOTS, 2)),
            pltpu.SemaphoreType.DMA((SLOTS, ratio)),
            pltpu.SemaphoreType.DMA((SLOTS, row_count, ratio)),
            pltpu.SemaphoreType.DMA((SLOTS, nbits)),
            pltpu.SemaphoreType.DMA((SLOTS, row_count)),
            pltpu.SemaphoreType.DMA((parts,)),
            pltpu.SemaphoreType.REGULAR((2,)),
            pltpu.SemaphoreType.REGULAR((nbits,)),
        ],
        compiler_params=pltpu.CompilerParams(
            collective_id=0, has_side_effects=True, vmem_limit_bytes=63 * 1024 * 1024
        ),
    )(pair, scale)
    return lax.psum(total, "ga")


def solution(mesh):
    placed = (P("row", None, "ga"), P("ga"))
    return jax.shard_map(
        local, mesh=mesh, in_specs=placed, out_specs=P("row", "col"), check_vma=False
    )
```

time: 853 us -> 404 us (0.47)
  waiting for transfers between devices: 571 us -> 0 us
  Pallas kernels: 0 us -> 383 us
  matrix products: 149 us -> 0 us
  other arithmetic: 45.8 us -> 1.31 us
  starting transfers between devices: 31.7 us -> 0 us
  local copies, waits for them, and re-layouts: 32.5 us -> 14.8 us
  between operations: 14.3 us -> 0.01 us
    all_gather x7 -> x0, waiting for transfers between devices: 568 us -> none  [local(): piece = lax.all_gather(own, 'row', axis=0, tiled=True)]
    pallas_call x0 -> x1, Pallas kernels: none -> 383 us  [local(): pl.pallas_call(functools.partial(kernel, (row_count, col_count, chunks, p...]
    dot_general x7 -> x0, matrix products: 149 us -> none  [contract(): lax.dot_general(left_rows, right_rows, (((1,), (1,)), ((), ())), precisio...]
    ppermute x14 -> x0, starting transfers between devices: 31.5 us -> none  [spread(): got = lax.ppermute(rows, ('row', 'col'), pairs)]
    select_n x7 -> x0, other arithmetic: 26.2 us -> none  [spread(): rows = jnp.where(away % (2 * bit) == bit, got, rows)]
    squeeze x7 -> x0, local copies, waits for them, and re-layouts: 25.1 us -> none  [local(): lax.dynamic_index_in_dim(paired, here_row // col_count, 1, keepdims=False)]
    mul x7 -> x0, other arithmetic: 19.5 us -> none  [local(): weighted = rows.reshape(local_k * bands, width) * scale[None, start:stop]]
    unnamed x42 -> x1, local copies, waits for them, and re-layouts: 1.21 us -> 14.8 us
  transfers between devices with their start and end apart: 21 -> 0, of which waited for: 7 -> 0; matrix products, arithmetic and copies ran while one was open for 19% -> 0% of each run, Pallas kernels for 0% -> 0%
where the time goes in v1:
time: 404 us; the launch traced here: 399 us
  Pallas kernels  383 us (95%)
  local copies, waits for them, and re-layouts  14.8 us (4%)
    pallas_call x1, Pallas kernels, local(): pl.pallas_call(functools.partial(kernel, (row_count, col_count, chunks, p...  383 us
    unnamed x1, local copies, waits for them, and re-layouts  14.8 us

profile of v1, /device:TPU:7, one launch (start us, length us, event | category | flops | bytes accessed | tf_op | source)
XLA Modules:
  0.0 399.2 jit_solution(15183475920959617150)
XLA Ops:
  0.0 1.3 broadcast_multiply_fusion
  1.3 383.1 %shard_map.28 = f32[1536,3072]{1,0:T(8,128)} custom-call(f32[8,2,4,24,3072]{4,3,2,1,0:T(8,128)} %bitcast.2, f32[12,1,256]{2,1,0:T(1,128)} %bitcast.3), custom_call_target="tpu_custom_call" | custom-call | tf_op jit(solution)/shard_map/pallas_call | solution.py:303
  384.5 14.8 %copy.4 = f32[1536,3072]{1,0:T(8,128)} copy(f32[1536,3072]{1,0:T(8,128)} %shard_map.28) | data formatting | bytes 37748736

commit v2 on v1

v2 whole, which is shorter than its diff:
```python
import functools
import math

import jax
import jax.numpy as jnp
from jax import lax
from jax.experimental import pallas as pl
from jax.experimental.pallas import tpu as pltpu
from jax.sharding import PartitionSpec as P

MESH = pl.DeviceIdType.MESH
WIDTH = 256
FLIGHT = 2
SLOTS = FLIGHT + 3
HOLD = 36
TILE = 512
ROWS = 768
TAKE = 10


def ring_at(place, count):
    far = place // (count // 2)
    return (1 - far) * 2 * place + far * (2 * (count - 1 - place) + 1)


def place_of(row, count):
    odd = row % 2
    return (1 - odd) * (row // 2) + odd * (count - 1 - row // 2)


def flip(col, bit):
    return col + bit * (1 - 2 * ((col // bit) % 2))


def split(x):
    high = x.astype(jnp.bfloat16)
    return high, (x - high.astype(jnp.float32)).astype(jnp.bfloat16)


def contract(rows, columns):
    return lax.dot_general(
        rows, columns, (((1,), (1,)), ((), ())), preferred_element_type=jnp.float32
    )


def kernel(
    sizes, pair_ref, coulomb_ref, total, weighted, last, right, left, columns,
    own_sem, ring_send, ring_recv, left_send, left_recv, ring_free, left_free,
):
    row_count, col_count, chunks, parts, total_k = sizes
    ratio = row_count // col_count
    per_class, bands = right.shape[2], right.shape[4]
    width = right.shape[5]
    here_row, here_col = lax.axis_index("row"), lax.axis_index("col")
    place = place_of(here_row, row_count)
    ahead = ring_at((place + 1) % row_count, row_count)
    behind = ring_at((place + row_count - 1) % row_count, row_count)
    home_col, home_class = here_row % col_count, here_row // col_count
    bits = [1 << b for b in range(int(math.log2(col_count)))]
    away = 0
    for bit in bits:
        away = away + bit * (((here_col // bit) + (home_col // bit)) % 2)
    half = row_count // 2
    period = half // FLIGHT
    group = row_count // parts
    ways = (ahead, behind)

    def hops(way, e):
        return half if way == e % 2 else half - 1

    def source_at(way, t):
        return ring_at((place + (row_count - t if way == 0 else t)) % row_count, row_count)

    def own_copies(g):
        s = g % SLOTS
        cut = pl.ds(pl.multiple_of(g * width, width), width)
        return (
            pltpu.make_async_copy(
                pair_ref.at[:, :, here_col, :, cut], right.at[s, here_row], own_sem.at[s, 0]
            ),
            pltpu.make_async_copy(
                pair_ref.at[:, home_class, home_col, :, cut], left.at[s, here_row], own_sem.at[s, 1]
            ),
        )

    def ring_copy(s, way, e, q):
        return pltpu.make_async_remote_copy(
            src_ref=right.at[s, q, :, e],
            dst_ref=right.at[s, q, :, e],
            send_sem=ring_send.at[s, way, e],
            recv_sem=ring_recv.at[s, q, e],
            device_id={"row": ways[way]},
            device_id_type=MESH,
        )

    def left_copy(src, s, q, b):
        return pltpu.make_async_remote_copy(
            src_ref=src,
            dst_ref=left.at[s, q],
            send_sem=left_send.at[s, b],
            recv_sem=left_recv.at[s, q],
            device_id={"col": flip(here_col, bits[b])},
            device_id_type=MESH,
        )

    def ring_event(g, t):
        s = g % SLOTS
        if t == 0:
            for copy in own_copies(g):
                copy.wait()

            @pl.when(g >= SLOTS)
            def _():
                for way in range(2):
                    pl.semaphore_wait(ring_free.at[way], 1)

        for turn in range(2):
            for way in range(2):
                for e in range(ratio):
                    if (way + e) % 2 != turn or t > hops(way, e):
                        continue
                    q = here_row if t == 0 else source_at(way, t)
                    if t > 0:
                        ring_copy(s, way, e, q).wait_recv()
                    if t < hops(way, e):
                        ring_copy(s, way, e, q).start()
        if t == 0:
            return

        @pl.when(away == 0)
        def _():
            for b in range(len(bits)):
                if t == 1:

                    @pl.when(g >= SLOTS)
                    def _():
                        pl.semaphore_wait(left_free.at[b], 1)

                for way in range(1 if t == half else 2):
                    q = source_at(way, t)
                    left_copy(right.at[s, q, :, home_class], s, q, b).start()

        if t == 1:

            @pl.when(g + 1 < chunks)
            def _():
                for copy in own_copies(g + 1):
                    copy.start()

    def relay_event(g, t):
        s = g % SLOTS

        @pl.when((away > 0) & (away % 2 == 0))
        def _():
            for way in range(1 if t == half else 2):
                q = source_at(way, t)
                left_copy(left.at[s, q], s, q, 0).wait_recv()
                for b, bit in enumerate(bits):

                    @pl.when(away % (2 * bit) == 0)
                    def _():
                        if t == 1 and way == 0:

                            @pl.when(g >= SLOTS)
                            def _():
                                pl.semaphore_wait(left_free.at[b], 1)

                        left_copy(left.at[s, q], s, q, b).start()

    def weigh(g):
        s = g % SLOTS
        rows = per_class * bands

        def clear(i, _):
            for p in range(parts):
                total[p, pl.ds(pl.multiple_of(i * 8, 8), 8), :] = jnp.zeros((8, total.shape[2]), jnp.float32)
            return 0

        @pl.when(g == 0)
        def _():
            lax.fori_loop(0, total.shape[1] // 8, clear, 0)

        scale = (2.0 * coulomb_ref[g]) / jnp.float32(total_k)

        @pl.when(away % 2 == 1)
        def _():
            for t in range(1, half + 1):
                for way in range(1 if t == half else 2):
                    q = source_at(way, t)
                    left_copy(left.at[s, q], s, q, 0).wait_recv()

        def fill(read):
            def one(q, _):
                high, low = split(read(q).reshape(rows, width) * scale)
                at = pl.ds(pl.multiple_of(q * rows, rows), rows)
                weighted[at, pl.ds(0, width)] = high
                weighted[at, pl.ds(width, width)] = high
                weighted[at, pl.ds(2 * width, width)] = low
                return 0

            lax.fori_loop(0, row_count, one, 0)

        @pl.when(away == 0)
        def _():
            fill(lambda q: right[s, q, :, home_class])

        @pl.when(away > 0)
        def _():
            fill(lambda q: left[s, q])

    def product(g, p):
        s = g % SLOTS
        block = group * per_class * ratio * bands
        high, low = split(right[s, pl.ds(p * group, group)].reshape(block, width))

        @pl.when(g == chunks - 1)
        def _():
            last[p, :, pl.ds(0, width)] = high
            last[p, :, pl.ds(width, width)] = low
            last[p, :, pl.ds(2 * width, width)] = high

        @pl.when(g < chunks - 1)
        def _():
            columns[:, pl.ds(0, width)] = high
            columns[:, pl.ds(width, width)] = low
            columns[:, pl.ds(2 * width, width)] = high
            tile = min(TILE, weighted.shape[0])

            def one(i, _):
                at = pl.ds(pl.multiple_of(i * tile, tile), tile)
                total[p, at, :] += contract(weighted[at, :], columns[...])
                return 0

            lax.fori_loop(0, weighted.shape[0] // tile, one, 0)

    def retire(g):
        s = g % SLOTS
        for way in range(2):
            for e in range(ratio):
                several = right.at[s, pl.ds(0, hops(way, e)), :, e]
                pltpu.make_async_copy(several, several, ring_send.at[s, way, e]).wait()
        several = left.at[s, pl.ds(0, row_count - 1)]
        for b, bit in enumerate(bits):

            @pl.when(away % (2 * bit) == 0)
            def _():
                pltpu.make_async_copy(several, several, left_send.at[s, b]).wait()

        @pl.when(g + SLOTS < chunks)
        def _():
            for way in range(2):
                pl.semaphore_signal(
                    ring_free.at[way], inc=1, device_id={"row": ways[1 - way]}, device_id_type=MESH
                )
            for b, bit in enumerate(bits):

                @pl.when(away % (2 * bit) == bit)
                def _():
                    pl.semaphore_signal(
                        left_free.at[b], inc=1, device_id={"col": flip(here_col, bit)}, device_id_type=MESH
                    )

    for copy in own_copies(0):
        copy.start()
    barrier = pltpu.get_barrier_semaphore()
    for row in (ahead, behind):
        pl.semaphore_signal(barrier, inc=1, device_id={"row": row}, device_id_type=MESH)
    for bit in bits:
        pl.semaphore_signal(barrier, inc=1, device_id={"col": flip(here_col, bit)}, device_id_type=MESH)
    pl.semaphore_wait(barrier, 2 + len(bits))

    def live(g, run):
        pl.when((g >= 0) & (g < chunks))(run)

    turns = [(i, d) for i in range(period) for d in range(FLIGHT + 1) if 0 < i + d * period <= half]

    def round_of(base, _):
        done = base - FLIGHT - 1
        for i in range(period):
            for d in range(FLIGHT + 1):
                t = i + d * period
                if 2 <= t <= half + 1:
                    live(base - d, functools.partial(relay_event, base - d, t - 1))
                if t <= half:
                    live(base - d, functools.partial(ring_event, base - d, t))
                if (i, d) == turns[0]:
                    live(done, functools.partial(weigh, done))
                for p in range(parts):
                    if turns[p * len(turns) // parts] == (i, d):
                        live(done, functools.partial(product, done, p))
        live(done, functools.partial(retire, done))
        return 0

    lax.fori_loop(0, chunks + FLIGHT + 1, round_of, 0)


def finish(total, weighted, last, out_ref):
    p, i = pl.program_id(0), pl.program_id(1)
    rows = out_ref.shape[0]
    at = pl.ds(pl.multiple_of(i * rows, rows), rows)
    out_ref[...] = total[p, at, :] + contract(weighted[at, :], last[p])


def local(pair_density, coulomb):
    row_count, col_count = lax.axis_size("row"), lax.axis_size("col")
    ratio = row_count // col_count
    local_k, bands, g_width = pair_density.shape
    total_k = local_k * row_count
    per_class = local_k // row_count
    width = math.gcd(WIDTH, g_width)
    chunks = g_width // width
    m, n = local_k * bands, total_k // col_count * bands
    piece = per_class * ratio * bands
    group = 1
    while group * piece % 256:
        group *= 2
    parts = row_count // group
    coulomb = coulomb.reshape(chunks, 1, width)
    pair = pair_density.reshape(per_class, ratio, col_count, bands, g_width)
    nbits = int(math.log2(col_count))
    f32, block = jnp.float32, group * piece
    kept = [
        jax.ShapeDtypeStruct((parts, m, block), f32),
        jax.ShapeDtypeStruct((m, 3 * width), jnp.bfloat16),
        jax.ShapeDtypeStruct((parts, block, 3 * width), jnp.bfloat16),
    ]
    sums = pl.pallas_call(
        functools.partial(kernel, (row_count, col_count, chunks, parts, total_k)),
        out_shape=[pltpu.VMEM(x.shape, x.dtype) for x in kept],
        in_specs=[pl.BlockSpec(memory_space=pl.ANY), pl.BlockSpec(memory_space=pltpu.VMEM)],
        out_specs=[pl.BlockSpec(memory_space=pltpu.VMEM)] * 3,
        scratch_shapes=[
            pltpu.VMEM((SLOTS, row_count, per_class, ratio, bands, width), f32),
            pltpu.VMEM((SLOTS, row_count, per_class, bands, width), f32),
            pltpu.VMEM((block, 3 * width), jnp.bfloat16),
            pltpu.SemaphoreType.DMA((SLOTS, 2)),
            pltpu.SemaphoreType.DMA((SLOTS, 2, ratio)),
            pltpu.SemaphoreType.DMA((SLOTS, row_count, ratio)),
            pltpu.SemaphoreType.DMA((SLOTS, nbits)),
            pltpu.SemaphoreType.DMA((SLOTS, row_count)),
            pltpu.SemaphoreType.REGULAR((2,)),
            pltpu.SemaphoreType.REGULAR((nbits,)),
        ],
        compiler_params=pltpu.CompilerParams(
            collective_id=0, has_side_effects=True, vmem_limit_bytes=HOLD * 1024 * 1024
        ),
    )(pair, coulomb)
    rows = min(ROWS, m)
    total = pl.pallas_call(
        finish,
        grid=(parts, m // rows),
        out_shape=jax.ShapeDtypeStruct((m, n), f32),
        in_specs=[pl.BlockSpec(memory_space=pltpu.VMEM)] * 3,
        out_specs=pl.BlockSpec((rows, block), lambda p, i: (i, p)),
        compiler_params=pltpu.CompilerParams(vmem_limit_bytes=TAKE * 1024 * 1024),
    )(*sums)
    return lax.psum(total, "ga")


def solution(mesh):
    placed = (P("row", None, "ga"), P("ga"))
    return jax.shard_map(
        local, mesh=mesh, in_specs=placed, out_specs=P("row", "col"), check_vma=False
    )
```

time: 404 us -> 386 us (0.955)
  local copies, waits for them, and re-layouts: 14.8 us -> 0 us
    unnamed x1 -> x0, local copies, waits for them, and re-layouts: 14.8 us -> none
    pallas_call x1, Pallas kernels: 383 us -> 370 us  [local(): pl.pallas_call(functools.partial(kernel, (row_count, col_count, chunks, p...]
    pallas_call x0 -> x1, Pallas kernels: none -> 11.2 us  [local(): pl.pallas_call(finish, grid=(parts, m // rows), out_shape=jax.ShapeDtypeS...]
where the time goes in v2:
time: 386 us; the launch traced here: 381 us
  Pallas kernels  381 us (99%)
    pallas_call x1, Pallas kernels, local(): pl.pallas_call(functools.partial(kernel, (row_count, col_count, chunks, p...  370 us
    pallas_call x1, Pallas kernels, local(): pl.pallas_call(finish, grid=(parts, m // rows), out_shape=jax.ShapeDtypeS...  11.2 us

profile of v2, /device:TPU:7, one launch (start us, length us, event | category | flops | bytes accessed | tf_op | source)
XLA Modules:
  0.0 381.1 jit_solution(12720937774927982234)
XLA Ops:
  0.0 369.8 %shard_map.28 = (f32[4,1536,768]{2,1,0:T(8,128)S(1)}, bf16[1536,768]{1,0:T(8,128)(2,1)S(1)}, bf16[4,768,768]{2,1,0:T(8,128)(2,1)S(1)}) custom-call(f32[8,2,4,24,3072]{4,3,2,1,0:T(8,128)} %bitcast.2, f32[12,1,256]{2,1,0:T(1,128)} %bitcast.3), custom_call_target="tpu_custom_call" | custom-call | tf_op jit(solution)/shard_map/pallas_call | solution.py:327
  369.9 11.2 %shard_map.29 = f32[1536,3072]{1,0:T(8,128)} custom-call(f32[4,1536,768]{2,1,0:T(8,128)S(1)} %get-tuple-element.8.total, bf16[1536,768]{1,0:T(8,128)(2,1)S(1)} %get-tuple-element.9.weighted, bf16[4,768,768]{2,1,0:T(8,128)(2,1)S(1)} %get-tuple-element.10.last), custom_call_target="tpu_custom_call" | custom-call | tf_op jit(solution)/shard_map/pallas_call | solution.py:349

commit v3 on v2

--- a/solution.py
+++ b/solution.py
@@ -11,11 +11,10 @@
 MESH = pl.DeviceIdType.MESH
 WIDTH = 256
 FLIGHT = 2
-SLOTS = FLIGHT + 3
-HOLD = 36
+SLOTS = FLIGHT + 2
 TILE = 512
 ROWS = 768
-TAKE = 10
+HOLD, TAKE = 36, 10
 
 
 def ring_at(place, count):
@@ -125,28 +124,27 @@
                     if t < hops(way, e):
                         ring_copy(s, way, e, q).start()
         if t == 0:
-            return
-
-        @pl.when(away == 0)
-        def _():
-            for b in range(len(bits)):
-                if t == 1:
-
-                    @pl.when(g >= SLOTS)
-                    def _():
-                        pl.semaphore_wait(left_free.at[b], 1)
-
-                for way in range(1 if t == half else 2):
-                    q = source_at(way, t)
-                    left_copy(right.at[s, q, :, home_class], s, q, b).start()
-
-        if t == 1:
 
             @pl.when(g + 1 < chunks)
             def _():
                 for copy in own_copies(g + 1):
                     copy.start()
 
+            return
+
+        @pl.when(away == 0)
+        def _():
+            for b in range(len(bits)):
+                if t == 1:
+
+                    @pl.when(g >= SLOTS)
+                    def _():
+                        pl.semaphore_wait(left_free.at[b], 1)
+
+                for way in range(1 if t == half else 2):
+                    q = source_at(way, t)
+                    left_copy(right.at[s, q, :, home_class], s, q, b).start()
+
     def relay_event(g, t):
         s = g % SLOTS
 
@@ -167,38 +165,32 @@
 
                         left_copy(left.at[s, q], s, q, b).start()
 
-    def weigh(g):
+    def sources(steps):
+        found = []
+        for t in steps:
+            if t == 0:
+                found.append(here_row)
+            for way in range(2 if 0 < t < half else t // half):
+                found.append(source_at(way, t))
+        return found
+
+    def weigh(g, steps):
         s = g % SLOTS
         rows = per_class * bands
-
-        def clear(i, _):
-            for p in range(parts):
-                total[p, pl.ds(pl.multiple_of(i * 8, 8), 8), :] = jnp.zeros((8, total.shape[2]), jnp.float32)
-            return 0
-
-        @pl.when(g == 0)
-        def _():
-            lax.fori_loop(0, total.shape[1] // 8, clear, 0)
-
         scale = (2.0 * coulomb_ref[g]) / jnp.float32(total_k)
 
         @pl.when(away % 2 == 1)
         def _():
-            for t in range(1, half + 1):
-                for way in range(1 if t == half else 2):
-                    q = source_at(way, t)
-                    left_copy(left.at[s, q], s, q, 0).wait_recv()
+            for q in sources(t for t in steps if t):
+                left_copy(left.at[s, q], s, q, 0).wait_recv()
 
         def fill(read):
-            def one(q, _):
+            for q in sources(steps):
                 high, low = split(read(q).reshape(rows, width) * scale)
                 at = pl.ds(pl.multiple_of(q * rows, rows), rows)
                 weighted[at, pl.ds(0, width)] = high
                 weighted[at, pl.ds(width, width)] = high
                 weighted[at, pl.ds(2 * width, width)] = low
-                return 0
-
-            lax.fori_loop(0, row_count, one, 0)
 
         @pl.when(away == 0)
         def _():
@@ -208,19 +200,40 @@
         def _():
             fill(lambda q: left[s, q])
 
+    def clear():
+        def one(i, _):
+            for p in range(parts):
+                total[p, pl.ds(pl.multiple_of(i * 8, 8), 8), :] = jnp.zeros((8, total.shape[2]), jnp.float32)
+            return 0
+
+        lax.fori_loop(0, total.shape[1] // 8, one, 0)
+
+    def keep(g, steps):
+        s = g % SLOTS
+        piece = per_class * ratio * bands
+        for q in sources(steps):
+            high, low = split(right[s, q].reshape(piece, width))
+            at = pl.ds(pl.multiple_of(q % group * piece, piece), piece)
+            last[q // group, at, pl.ds(0, width)] = high
+            last[q // group, at, pl.ds(width, width)] = low
+            last[q // group, at, pl.ds(2 * width, width)] = high
+
+    def prepare(g):
+        weigh(g, range(half - 1))
+        pl.when(g == 0)(clear)
+        pl.when(g == chunks - 1)(functools.partial(keep, g, range(half)))
+
+    def complete(g):
+        weigh(g, range(half - 1, half + 1))
+        pl.when(g == chunks - 1)(functools.partial(keep, g, range(half, half + 1)))
+
     def product(g, p):
         s = g % SLOTS
         block = group * per_class * ratio * bands
-        high, low = split(right[s, pl.ds(p * group, group)].reshape(block, width))
-
-        @pl.when(g == chunks - 1)
-        def _():
-            last[p, :, pl.ds(0, width)] = high
-            last[p, :, pl.ds(width, width)] = low
-            last[p, :, pl.ds(2 * width, width)] = high
 
         @pl.when(g < chunks - 1)
         def _():
+            high, low = split(right[s, pl.ds(p * group, group)].reshape(block, width))
             columns[:, pl.ds(0, width)] = high
             columns[:, pl.ds(width, width)] = low
             columns[:, pl.ds(2 * width, width)] = high
@@ -272,26 +285,29 @@
     def live(g, run):
         pl.when((g >= 0) & (g < chunks))(run)
 
-    turns = [(i, d) for i in range(period) for d in range(FLIGHT + 1) if 0 < i + d * period <= half]
+    turns = [(i, d) for i in range(1, period) for d in range(FLIGHT)]
 
     def round_of(base, _):
-        done = base - FLIGHT - 1
+        done = base - FLIGHT
         for i in range(period):
             for d in range(FLIGHT + 1):
                 t = i + d * period
                 if 2 <= t <= half + 1:
                     live(base - d, functools.partial(relay_event, base - d, t - 1))
+            for d in range(FLIGHT + 1):
+                t = i + d * period
                 if t <= half:
                     live(base - d, functools.partial(ring_event, base - d, t))
                 if (i, d) == turns[0]:
-                    live(done, functools.partial(weigh, done))
+                    live(done, functools.partial(complete, done))
                 for p in range(parts):
                     if turns[p * len(turns) // parts] == (i, d):
                         live(done, functools.partial(product, done, p))
         live(done, functools.partial(retire, done))
+        live(done + 1, functools.partial(prepare, done + 1))
         return 0
 
-    lax.fori_loop(0, chunks + FLIGHT + 1, round_of, 0)
+    lax.fori_loop(0, chunks + FLIGHT, round_of, 0)
 
 
 def finish(total, weighted, last, out_ref):

time: 386 us -> 384 us (level)
  no operation moved by 1% of the time
where the time goes in v3:
time: 384 us; the launch traced here: 378 us
  Pallas kernels  378 us (98%)
    pallas_call x1, Pallas kernels, local(): pl.pallas_call(functools.partial(kernel, (row_count, col_count, chunks, p...  367 us
    pallas_call x1, Pallas kernels, local(): pl.pallas_call(finish, grid=(parts, m // rows), out_shape=jax.ShapeDtypeS...  11.2 us

profile of v3, /device:TPU:7, one launch (start us, length us, event | category | flops | bytes accessed | tf_op | source)
XLA Modules:
  0.0 377.8 jit_solution(404070812564520895)
XLA Ops:
  0.0 366.6 %shard_map.28 = (f32[4,1536,768]{2,1,0:T(8,128)S(1)}, bf16[1536,768]{1,0:T(8,128)(2,1)S(1)}, bf16[4,768,768]{2,1,0:T(8,128)(2,1)S(1)}) custom-call(f32[8,2,4,24,3072]{4,3,2,1,0:T(8,128)} %bitcast.2, f32[12,1,256]{2,1,0:T(1,128)} %bitcast.3), custom_call_target="tpu_custom_call" | custom-call | tf_op jit(solution)/shard_map/pallas_call | solution.py:343
  366.6 11.2 %shard_map.29 = f32[1536,3072]{1,0:T(8,128)} custom-call(f32[4,1536,768]{2,1,0:T(8,128)S(1)} %get-tuple-element.8.total, bf16[1536,768]{1,0:T(8,128)(2,1)S(1)} %get-tuple-element.9.weighted, bf16[4,768,768]{2,1,0:T(8,128)(2,1)S(1)} %get-tuple-element.10.last), custom_call_target="tpu_custom_call" | custom-call | tf_op jit(solution)/shard_map/pallas_call | solution.py:365

commit v4 on v3

--- a/solution.py
+++ b/solution.py
@@ -12,7 +12,7 @@
 WIDTH = 256
 FLIGHT = 2
 SLOTS = FLIGHT + 2
-TILE = 512
+TILE = 768
 ROWS = 768
 HOLD, TAKE = 36, 10
 
@@ -224,8 +224,9 @@
         pl.when(g == chunks - 1)(functools.partial(keep, g, range(half)))
 
     def complete(g):
-        weigh(g, range(half - 1, half + 1))
         pl.when(g == chunks - 1)(functools.partial(keep, g, range(half, half + 1)))
+        weigh(g, range(half - 1, half))
+        weigh(g, range(half, half + 1))
 
     def product(g, p):
         s = g % SLOTS

time: 384 us -> 383 us (level)
  no operation moved by 1% of the time
where the time goes in v4:
time: 383 us; the launch traced here: 377 us
  Pallas kernels  377 us (98%)
    pallas_call x1, Pallas kernels, local(): pl.pallas_call(functools.partial(kernel, (row_count, col_count, chunks, p...  366 us
    pallas_call x1, Pallas kernels, local(): pl.pallas_call(finish, grid=(parts, m // rows), out_shape=jax.ShapeDtypeS...  11.2 us

profile of v4, /device:TPU:7, one launch (start us, length us, event | category | flops | bytes accessed | tf_op | source)
XLA Modules:
  0.0 377.4 jit_solution(7784572383597618458)
XLA Ops:
  0.0 366.2 %shard_map.28 = (f32[4,1536,768]{2,1,0:T(8,128)S(1)}, bf16[1536,768]{1,0:T(8,128)(2,1)S(1)}, bf16[4,768,768]{2,1,0:T(8,128)(2,1)S(1)}) custom-call(f32[8,2,4,24,3072]{4,3,2,1,0:T(8,128)} %bitcast.2, f32[12,1,256]{2,1,0:T(1,128)} %bitcast.3), custom_call_target="tpu_custom_call" | custom-call | tf_op jit(solution)/shard_map/pallas_call | solution.py:344
  366.2 11.2 %shard_map.29 = f32[1536,3072]{1,0:T(8,128)} custom-call(f32[4,1536,768]{2,1,0:T(8,128)S(1)} %get-tuple-element.8.total, bf16[1536,768]{1,0:T(8,128)(2,1)S(1)} %get-tuple-element.9.weighted, bf16[4,768,768]{2,1,0:T(8,128)(2,1)S(1)} %get-tuple-element.10.last), custom_call_target="tpu_custom_call" | custom-call | tf_op jit(solution)/shard_map/pallas_call | solution.py:366
